TPU v7x, 32 devices: a whole 2x2x4 slice. The times are simulated.
32 devices in a mesh: dp: 16 (over z, y, core), fsdp: 2 (over x).
Axes of the slice: x: 2, y: 2, z: 4, core: 2. Of those that a mesh axis runs over, the one named last changes fastest.
Arguments:
- patches: bfloat16 [16384, 768], P(('dp', 'fsdp')), may hold values from -6 to 6
- cotangent: bfloat16 [16384, 768], P(('dp', 'fsdp')), may hold values from -6 to 6
- lengths: int32 [32, 4], P(('dp', 'fsdp')), may hold values from 0 to 512, as said below
- arrange: int32 [16384], P(('dp', 'fsdp')), may hold values from 0 to 511, as said below
- first_gain: bfloat16 [768], P('dp'), may hold values from 0.3984375 to 1.59375
- first_shift: bfloat16 [768], P('dp'), may hold values from -1.5 to 1.5
- project_weight: bfloat16 [768, 2304], P('dp', 'fsdp'), may hold values from -0.21875 to 0.21875
- query_bias: bfloat16 [768], P('dp'), may hold values from -1.5 to 1.5
- value_bias: bfloat16 [768], P('dp'), may hold values from -1.5 to 1.5
- output_weight: bfloat16 [768, 768], P('dp', 'fsdp'), may hold values from -1.75 to 1.75
- output_bias: bfloat16 [768], P('dp'), may hold values from -1.5 to 1.5
- second_gain: bfloat16 [768], P('dp'), may hold values from 0.3984375 to 1.59375
- second_shift: bfloat16 [768], P('dp'), may hold values from -1.5 to 1.5
- up_weight: bfloat16 [768, 3072], P('dp', 'fsdp'), may hold values from -0.21875 to 0.21875
- up_bias: bfloat16 [3072], P('dp'), may hold values from -1.5 to 1.5
- down_weight: bfloat16 [3072, 768], P('dp', 'fsdp'), may hold values from -0.109375 to 0.109375
- down_bias: bfloat16 [768], P('dp'), may hold values from -1.5 to 1.5
Outputs:
- encoded: bfloat16 [16384, 768], P(('dp', 'fsdp'))
- grad_patches: bfloat16 [16384, 768], P(('dp', 'fsdp'))
- grad_first_gain: float32 [768], P('dp')
- grad_first_shift: float32 [768], P('dp')
- grad_project_weight: float32 [768, 2304], P('dp', 'fsdp')
- grad_query_bias: float32 [768], P('dp')
- grad_value_bias: float32 [768], P('dp')
- grad_output_weight: float32 [768, 768], P('dp', 'fsdp')
- grad_output_bias: float32 [768], P('dp')
- grad_second_gain: float32 [768], P('dp')
- grad_second_shift: float32 [768], P('dp')
- grad_up_weight: float32 [768, 3072], P('dp', 'fsdp')
- grad_up_bias: float32 [3072], P('dp')
- grad_down_weight: float32 [3072, 768], P('dp', 'fsdp')
- grad_down_bias: float32 [768], P('dp')
Inputs may be any that keep to these rules, and one draw needn't show every extreme that they name: Each block's 4 lengths sum to at least 384 and at most 512; slots may be empty; in every draw some block holds a single sequence of 512 rows. `arrange`: each block's 512 entries are a permutation of 0 to 511.
All inputs are finite; a program needn't handle non-finite values.
Results may differ from a plain program's by a relative error of at most 0.012.
Values may be sent and summed in bfloat16 or wider, within the bound.
A program may use at most 128 MiB of HBM per device.

v0:
```python
import jax
import jax.numpy as jnp
from jax import lax
from jax.sharding import PartitionSpec as P

HEADS = 12
HEAD = 64
NORM_EPSILON = 1e-12
MASK_VALUE = -1e30
ROOT_HALF = 0.7071067811865476


def norm_rows(values, norm_gain, norm_shift):
    center = values - jnp.mean(values, axis=-1, keepdims=True)
    spread = jnp.mean(center * center, axis=-1, keepdims=True)
    return center * lax.rsqrt(spread + NORM_EPSILON) * norm_gain + norm_shift


def gelu_exact(values):
    return 0.5 * values * (1.0 + lax.erf(values * ROOT_HALF))


def slot_labels(lengths, arrange):
    total_rows = arrange.shape[0]
    slot_ends = jnp.cumsum(lengths[0])
    position = jnp.arange(total_rows, dtype=jnp.int32)
    slot_index = jnp.sum((position[:, None] >= slot_ends[None, :]).astype(jnp.int32), axis=1)
    return jnp.zeros((total_rows,), jnp.int32).at[arrange].set(slot_index)


def matmul(left_side, right_side, pattern):
    return jnp.einsum(pattern, left_side, right_side, preferred_element_type=jnp.float32)


def column_sums(values):
    return jnp.sum(values.astype(jnp.float32), axis=0)


def gather_matrix(block, n_dp, n_fsdp):
    rows, cols = block.shape
    every = lax.all_gather(block, ("dp", "fsdp"), axis=0, tiled=False)
    every = every.reshape(n_dp, n_fsdp, rows, cols).transpose(0, 2, 1, 3)
    return every.reshape(n_dp * rows, n_fsdp * cols)


def scatter_matrix(grad):
    part = lax.psum_scatter(grad.astype(jnp.bfloat16), "dp", scatter_dimension=0, tiled=True)
    part = lax.psum_scatter(part, "fsdp", scatter_dimension=1, tiled=True)
    return part.astype(jnp.float32)


def local(
    n_dp,
    n_fsdp,
    patches,
    cotangent,
    lengths,
    arrange,
    first_gain,
    first_shift,
    project_weight,
    query_bias,
    value_bias,
    output_weight,
    output_bias,
    second_gain,
    second_shift,
    up_weight,
    up_bias,
    down_weight,
    down_bias,
):
    arrived, cot_rows = (
        lax.all_to_all(patches, "dp", split_axis=0, concat_axis=0, tiled=True),
        lax.all_to_all(cotangent, "dp", split_axis=0, concat_axis=0, tiled=True),
    )
    total_rows, width = patches.shape
    labels = slot_labels(lengths, arrange)
    live_rows = (labels < lengths.shape[1]).astype(jnp.float32)[:, None]
    vector_parts = (
        first_gain,
        first_shift,
        query_bias,
        value_bias,
        output_bias,
        second_gain,
        second_shift,
        up_bias,
        down_bias,
    )
    widths = [v.shape[0] for v in vector_parts]
    packed = lax.all_gather(jnp.concatenate(vector_parts)[None], "dp", axis=0, tiled=True)
    vectors = []
    offset = 0
    for w in widths:
        vectors.append(packed[:, offset : offset + w].reshape(-1).astype(jnp.float32))
        offset += w
    (
        gain_one,
        shift_one,
        query_full,
        value_full,
        outbias_full,
        gain_two,
        shift_two,
        upbias_full,
        downbias_full,
    ) = vectors
    project_full = gather_matrix(project_weight, n_dp, n_fsdp)
    output_full = gather_matrix(output_weight, n_dp, n_fsdp)
    up_full = gather_matrix(up_weight, n_dp, n_fsdp)
    down_full = gather_matrix(down_weight, n_dp, n_fsdp)
    inputs = arrived.astype(jnp.float32)
    normed_one = norm_rows(inputs, gain_one, shift_one)
    normed_low = normed_one.astype(jnp.bfloat16)
    joint = jnp.dot(normed_low, project_full, preferred_element_type=jnp.float32)
    queries = (joint[:, :width] + query_full).astype(jnp.bfloat16).reshape(total_rows, HEADS, HEAD)
    key_rows = joint[:, width : 2 * width].astype(jnp.bfloat16).reshape(total_rows, HEADS, HEAD)
    value_rows = (
        (joint[:, 2 * width :] + value_full).astype(jnp.bfloat16).reshape(total_rows, HEADS, HEAD)
    )
    score_scale = HEAD ** (-0.5)
    visible = labels[:, None] == labels[None, :]

    def block_scores():
        raw_scores = matmul(queries, key_rows, "qhe,khe->hqk") * score_scale
        return jnp.where(visible[None], raw_scores, MASK_VALUE)

    scores = block_scores()
    top_score = jnp.max(scores, axis=-1, keepdims=True)
    weights = jnp.exp(scores - top_score)
    totals = jnp.sum(weights, axis=-1, keepdims=True)
    prob_low = (weights / totals).astype(jnp.bfloat16)
    mixed_rows = matmul(prob_low, value_rows, "hqk,khe->qhe")
    log_totals = top_score + jnp.log(totals)
    attended = mixed_rows.astype(jnp.bfloat16).reshape(total_rows, width)
    attn_out = jnp.dot(attended, output_full, preferred_element_type=jnp.float32) + outbias_full
    hidden = inputs + attn_out
    normed_two = norm_rows(hidden, gain_two, shift_two)
    normed_two_low = normed_two.astype(jnp.bfloat16)
    pre_act = jnp.dot(normed_two_low, up_full, preferred_element_type=jnp.float32) + upbias_full
    activated = gelu_exact(pre_act).astype(jnp.bfloat16)
    branch = jnp.dot(activated, down_full, preferred_element_type=jnp.float32) + downbias_full
    encoded_rows = live_rows * (hidden + branch)
    encoded_back = lax.all_to_all(
        encoded_rows.astype(jnp.bfloat16), "dp", split_axis=0, concat_axis=0, tiled=True
    )
    grad_out = live_rows * cot_rows.astype(jnp.float32)
    grad_branch = grad_out.astype(jnp.bfloat16)
    grad_down = matmul(activated, grad_branch, "tf,td->fd")
    grad_downbias = column_sums(grad_branch)
    grad_activ = matmul(grad_branch, down_full, "td,fd->tf")
    grad_pre = jax.vjp(gelu_exact, pre_act)[1](grad_activ)[0].astype(jnp.bfloat16)
    grad_up = matmul(normed_two_low, grad_pre, "td,tf->df")
    grad_upbias = column_sums(grad_pre)
    grad_normed_two = matmul(grad_pre, up_full, "tf,df->td")
    norm_pull_two = jax.vjp(norm_rows, hidden, gain_two, shift_two)[1]
    grad_hidden_part, grad_gain_two, grad_shift_two = norm_pull_two(grad_normed_two)
    grad_hidden = grad_out + grad_hidden_part
    down_low, up_low = (grad_down.astype(jnp.bfloat16), grad_up.astype(jnp.bfloat16))
    grad_hidden, down_low, up_low = lax.optimization_barrier((grad_hidden, down_low, up_low))
    down_part = scatter_matrix(down_low)
    up_part = scatter_matrix(up_low)
    grad_attn = grad_hidden.astype(jnp.bfloat16)
    grad_output = matmul(attended, grad_attn, "td,te->de")
    grad_outbias = column_sums(grad_attn)
    grad_attended = (
        matmul(grad_attn, output_full, "te,de->td")
        .astype(jnp.bfloat16)
        .reshape(total_rows, HEADS, HEAD)
    )
    output_low = grad_output.astype(jnp.bfloat16)
    grad_attended, output_low = lax.optimization_barrier((grad_attended, output_low))
    output_part = scatter_matrix(output_low)
    scores = block_scores()
    prob_full = jnp.exp(scores - log_totals)
    prob_low = prob_full.astype(jnp.bfloat16)
    value_grad = matmul(prob_low, grad_attended, "hqk,qhe->khe")
    grad_prob = matmul(grad_attended, value_rows, "qhe,khe->hqk")
    inner = jnp.sum(prob_full * grad_prob, axis=-1, keepdims=True)
    grad_scores = (prob_full * (grad_prob - inner)).astype(jnp.bfloat16)
    query_grad = matmul(grad_scores, key_rows, "hqk,khe->qhe") * score_scale
    key_grad = matmul(grad_scores, queries, "hqk,qhe->khe") * score_scale
    grad_queries = query_grad.astype(jnp.bfloat16).reshape(total_rows, width)
    grad_keys = key_grad.reshape(total_rows, width).astype(jnp.bfloat16)
    grad_values = value_grad.reshape(total_rows, width).astype(jnp.bfloat16)
    grad_joint = jnp.concatenate([grad_queries, grad_keys, grad_values], axis=1)
    grad_project = matmul(normed_low, grad_joint, "td,tf->df")
    grad_querybias = column_sums(grad_queries)
    grad_valuebias = column_sums(grad_values)
    project_part = scatter_matrix(grad_project)
    grad_normed_one = matmul(grad_joint, project_full, "tf,df->td")
    norm_pull_one = jax.vjp(norm_rows, inputs, gain_one, shift_one)[1]
    grad_input_part, grad_gain_one, grad_shift_one = norm_pull_one(grad_normed_one)
    grad_inputs = grad_hidden + grad_input_part
    grad_back = lax.all_to_all(
        grad_inputs.astype(jnp.bfloat16), "dp", split_axis=0, concat_axis=0, tiled=True
    )
    vector_grads = (
        grad_gain_one,
        grad_shift_one,
        grad_querybias,
        grad_valuebias,
        grad_outbias,
        grad_gain_two,
        grad_shift_two,
        grad_upbias,
        grad_downbias,
    )
    stacked = jnp.concatenate([g.reshape(n_dp, -1) for g in vector_grads], axis=1)
    stacked = stacked + lax.ppermute(
        stacked, "fsdp", [(i, (i + 1) % n_fsdp) for i in range(n_fsdp)]
    )
    mine = lax.psum_scatter(stacked, "dp", scatter_dimension=0, tiled=True)[0]
    sums = []
    offset = 0
    for w in widths:
        sums.append(mine[offset : offset + w])
        offset += w
    (
        g_gain_one,
        g_shift_one,
        g_querybias,
        g_valuebias,
        g_outbias,
        g_gain_two,
        g_shift_two,
        g_upbias,
        g_downbias,
    ) = sums
    return (
        encoded_back,
        grad_back,
        g_gain_one,
        g_shift_one,
        project_part,
        g_querybias,
        g_valuebias,
        output_part,
        g_outbias,
        g_gain_two,
        g_shift_two,
        up_part,
        g_upbias,
        down_part,
        g_downbias,
    )


def solution(mesh):
    n_dp, n_fsdp = (mesh.shape["dp"], mesh.shape["fsdp"])
    rows = P(("dp", "fsdp"), None)
    matrix = P("dp", "fsdp")
    vector = P("dp")

    def step(*args):
        return local(n_dp, n_fsdp, *args)

    return jax.shard_map(
        step,
        mesh=mesh,
        in_specs=(
            rows,
            rows,
            rows,
            P(("dp", "fsdp")),
            vector,
            vector,
            matrix,
            vector,
            vector,
            matrix,
            vector,
            vector,
            vector,
            matrix,
            vector,
            matrix,
            vector,
        ),
        out_specs=(
            rows,
            rows,
            vector,
            vector,
            matrix,
            vector,
            vector,
            matrix,
            vector,
            vector,
            vector,
            matrix,
            vector,
            matrix,
            vector,
        ),
        check_vma=False,
    )
```

profile of v0, /device:TPU:0, one launch (start us, length us, event | category | flops | bytes accessed | tf_op | source)
XLA Modules:
  0.0 716.6 jit_solution(4727964703437797031)
XLA Ops:
  9.5 7.4 %all-to-all-start = ((bf16[16,32,768]{2,1,0:T(8,128)(2,1)}), bf16[16,32,768]{2,1,0:T(8,128)(2,1)S(1)}, u32[]{:S(2)}, u32[]{:S(2)}) async-start(bf16[16,32,768]{2,1,0:T(8,128)(2,1)} %bitcast.168), calls=%async_computation | async-start | bytes 1572864 | tf_op jit(solution)/shard_map/all_to_all | solution.py:74
  21.6 14.6 %all-to-all-done = bf16[16,32,768]{2,1,0:T(8,128)(2,1)S(1)} async-done(((bf16[16,32,768]{2,1,0:T(8,128)(2,1)}), bf16[16,32,768]{2,1,0:T(8,128)(2,1)S(1)}, u32[]{:S(2)}, u32[]{:S(2)}) %all-to-all-start) | async-done | bytes 786464 | tf_op jit(solution)/shard_map/all_to_all | solution.py:74
  36.1 5.6 all-to-all-start.2
  43.6 68.6 %all-reduce = bf16[9216]{0:T(1024)(128)(2,1)S(1)} all-reduce(bf16[9216]{0:T(1024)(128)(2,1)S(1)} %dynamic-update-slice), channel_id=2, replica_groups=mesh['dp'=16,'fsdp'=2] {'dp'}, use_global_device_ids=true, to_apply=%add | all-reduce | flops 9216 | bytes 36864
  119.8 16.1 %all-gather.10.cloned.1.call-done = bf16[1536,1152]{1,0:T(8,128)(2,1)} async-done(((bf16[48,1152]{1,0:T(8,128)(2,1)}), bf16[1536,1152]{1,0:T(8,128)(2,1)}) %all-gather.10.cloned.1.call-update) | async-done | bytes 3538960 | tf_op jit(solution)/shard_map/all_gather | solution.py:41
  135.9 4.7 copy.68
  160.8 40.3 %all-gather.14.cloned.1.call-done = bf16[1536,1536]{1,0:T(8,128)(2,1)} async-done(((bf16[48,1536]{1,0:T(8,128)(2,1)}), bf16[1536,1536]{1,0:T(8,128)(2,1)}) %all-gather.14.cloned.1.call-update) | async-done | bytes 4718608 | tf_op jit(solution)/shard_map/all_gather | solution.py:41
  201.2 9.4 %copy.74 = bf16[16,2,48,1536]{3,1,2,0:T(2,128)(2,1)} copy(bf16[16,2,48,1536]{3,2,1,0:T(8,128)(2,1)} %bitcast.143) | data formatting | bytes 9437184 | tf_op jit(solution)/shard_map/reshape | solution.py:42
  210.5 5.7 copy.92
  216.3 49.5 %all-gather.16.cloned.1.call-done = bf16[6144,384]{1,0:T(8,128)(2,1)} async-done(((bf16[192,384]{1,0:T(8,128)(2,1)}), bf16[6144,384]{1,0:T(8,128)(2,1)}) %all-gather.16.cloned.1.call-update) | async-done | bytes 4718608 | tf_op jit(solution)/shard_map/all_gather | solution.py:41
  265.8 9.6 %copy.75 = bf16[16,2,192,384]{3,1,2,0:T(2,128)(2,1)} copy(bf16[16,2,192,384]{3,2,1,0:T(8,128)(2,1)} %bitcast.144) | data formatting | bytes 9437184 | tf_op jit(solution)/shard_map/reshape | solution.py:42
  281.9 6.7 convert_reduce_fusion
  292.6 4.9 convolution_convert_fusion.1
  301.5 4.5 convolution_convert_fusion.2
  313.2 9.0 %convert_reduce_fusion.4 = (f32[12,64]{1,0:T(8,128)S(1)}, bf16[12,64,512]{2,1,0:T(8,128)(2,1)}) fusion(bf16[512,12,64]{0,2,1:T(8,128)(2,1)} %bitcast.155, f32[12,512]{1,0:T(8,128)S(1)} %log_add_fusion, f32[12,512,512]{1,2,0:T(8,128)} %copy-done, pred[512,512]{0,1:T(8,128)(4,1)S(1)} %broadcast_compare_fusion), kind=kOutput, calls=%fused_computation.51 | convolution fusion | flops 416414976 | bytes 14445568 | tf_op jit(solution)/shard_map/hqk,qhe->khe/dot_general | solution.py:32
  322.2 9.6 %multiply_reduce_fusion = (f32[12,512]{1,0:T(8,128)S(1)}, f32[12,512,512]{1,2,0:T(8,128)}) fusion(f32[12,512]{1,0:T(8,128)S(1)} %log_add_fusion, f32[12,512,512]{1,2,0:T(8,128)} %copy-done, pred[512,512]{0,1:T(8,128)(4,1)S(1)} %broadcast_compare_fusion, bf16[512,12,64]{0,2,1:T(8,128)(2,1)S(1)} %bitcast.156, bf16[512,12,64]{0,2,1:T(8,128)(2,1)S(1)} %bitcast.154), kind=kOutput, calls=%fused_computation.2 | convolution fusion | flops 418375680 | bytes 27049984 | tf_op jit(solution)/shard_map/qhe,khe->hqk/dot_general | solution.py:32
  331.7 7.1 multiply_convert_fusion
  344.1 5.0 fusion.44
  357.8 6.9 multiply_convert_fusion.5
  368.7 39.1 %reduce-scatter.17.cloned.1.call-done = bf16[48,768]{1,0:T(8,128)(2,1)} async-done(((bf16[768,768]{1,0:T(8,128)(2,1)}), bf16[48,768]{1,0:T(8,128)(2,1)}) %reduce-scatter.17.cloned.1.call-update) | async-done | bytes 73744 | tf_op jit(solution)/shard_map/reduce_scatter | solution.py:47
  409.5 69.1 %reduce-scatter.15.cloned.1.call-done = bf16[48,2304]{1,0:T(8,128)(2,1)} async-done(((bf16[768,2304]{1,0:T(8,128)(2,1)}), bf16[48,2304]{1,0:T(8,128)(2,1)}) %reduce-scatter.15.cloned.1.call-update) | async-done | bytes 221200 | tf_op jit(solution)/shard_map/reduce_scatter | solution.py:47
  484.3 72.6 %reduce-scatter.23.cloned.1.call-done = bf16[192,768]{1,0:T(8,128)(2,1)} async-done(((bf16[3072,768]{1,0:T(8,128)(2,1)}), bf16[192,768]{1,0:T(8,128)(2,1)}) %reduce-scatter.23.cloned.1.call-update) | async-done | bytes 294928 | tf_op jit(solution)/shard_map/reduce_scatter | solution.py:47
  558.9 76.8 %reduce-scatter.19.cloned.1.call-done = bf16[48,3072]{1,0:T(8,128)(2,1)} async-done(((bf16[768,3072]{1,0:T(8,128)(2,1)}), bf16[48,3072]{1,0:T(8,128)(2,1)}) %reduce-scatter.19.cloned.1.call-update) | async-done | bytes 294928 | tf_op jit(solution)/shard_map/reduce_scatter | solution.py:47
  640.5 57.7 %all-reduce.1 = f32[16,576]{1,0:T(8,128)S(1)} all-reduce(f32[16,576]{1,0:T(8,128)S(1)} %add.163), channel_id=7, replica_groups=mesh['dp'=16,'fsdp'=2] {'dp'}, use_global_device_ids=true, to_apply=%region_23.24.clone | all-reduce | flops 9216 | bytes 73728
  (197 shorter events, 100.4 us)
Async XLA Ops:
  7.2 36.0 %copy-start.29 = (bf16[48]{0:T(256)(128)(2,1)S(1)}, bf16[48]{0:T(256)(128)(2,1)}, u32[]{:S(2)}) copy-start(bf16[48]{0:T(256)(128)(2,1)} %param.33) | copy-start | bytes 292
  7.2 36.0 %copy-start.28 = (bf16[192]{0:T(256)(128)(2,1)S(1)}, bf16[192]{0:T(256)(128)(2,1)}, u32[]{:S(2)}) copy-start(bf16[192]{0:T(256)(128)(2,1)} %param.31) | copy-start | bytes 1156
  7.2 36.0 %copy-start.27 = (bf16[48]{0:T(256)(128)(2,1)S(1)}, bf16[48]{0:T(256)(128)(2,1)}, u32[]{:S(2)}) copy-start(bf16[48]{0:T(256)(128)(2,1)} %param.29) | copy-start | bytes 292
  7.2 36.0 %copy-start.26 = (bf16[48]{0:T(256)(128)(2,1)S(1)}, bf16[48]{0:T(256)(128)(2,1)}, u32[]{:S(2)}) copy-start(bf16[48]{0:T(256)(128)(2,1)} %param.28) | copy-start | bytes 292
  7.2 36.0 %copy-start.25 = (bf16[48]{0:T(256)(128)(2,1)S(1)}, bf16[48]{0:T(256)(128)(2,1)}, u32[]{:S(2)}) copy-start(bf16[48]{0:T(256)(128)(2,1)} %param.27) | copy-start | bytes 292
  7.2 36.0 %copy-start.24 = (bf16[48]{0:T(256)(128)(2,1)S(1)}, bf16[48]{0:T(256)(128)(2,1)}, u32[]{:S(2)}) copy-start(bf16[48]{0:T(256)(128)(2,1)} %param.25) | copy-start | bytes 292
  7.3 109.1 %all-gather.12.cloned.1.call-start = ((), (), s32[]{:S(2)}) async-start(), calls=%async_computation.18 | async-start | bytes 1216512 | tf_op jit(solution)/shard_map/all_gather | solution.py:41
  8.0 127.9 %all-gather.10.cloned.1.call-start = ((), (), s32[]{:S(2)}) async-start(), calls=%async_computation.17 | async-start | bytes 3649536 | tf_op jit(solution)/shard_map/all_gather | solution.py:41
  8.8 192.4 %all-gather.14.cloned.1.call-start = ((), (), s32[]{:S(2)}) async-start(), calls=%async_computation.19 | async-start | bytes 4866048 | tf_op jit(solution)/shard_map/all_gather | solution.py:41
  9.5 26.6 %all-to-all-start = ((bf16[16,32,768]{2,1,0:T(8,128)(2,1)}), bf16[16,32,768]{2,1,0:T(8,128)(2,1)S(1)}, u32[]{:S(2)}, u32[]{:S(2)}) async-start(bf16[16,32,768]{2,1,0:T(8,128)(2,1)} %bitcast.168), calls=%async_computation | async-start | bytes 1572864 | tf_op jit(solution)/shard_map/all_to_all | solution.py:74
  16.9 248.9 %all-gather.16.cloned.1.call-start = ((), (), s32[]{:S(2)}) async-start(), calls=%async_computation.20 | async-start | bytes 4866048 | tf_op jit(solution)/shard_map/all_gather | solution.py:41
  36.1 77.8 %all-to-all-start.2 = ((bf16[16,32,768]{2,1,0:T(8,128)(2,1)}), bf16[16,32,768]{2,1,0:T(8,128)(2,1)S(1)}, u32[]{:S(2)}, u32[]{:S(2)}) async-start(bf16[16,32,768]{2,1,0:T(8,128)(2,1)} %bitcast.169), calls=%async_computation.2 | async-start | bytes 1572864 | tf_op jit(solution)/shard_map/all_to_all | solution.py:75
  41.8 366.0 %reduce-scatter.17.cloned.1.call-start = ((), (), s32[]{:S(2)}) async-start(), calls=%async_computation.13 | async-start | bytes 1253376 | tf_op jit(solution)/shard_map/reduce_scatter | solution.py:47
  160.5 137.0 %copy-start.5 = (f32[512,768]{1,0:T(8,128)}, f32[512,768]{1,0:T(8,128)S(1)}, u32[]{:S(2)}) copy-start(f32[512,768]{1,0:T(8,128)S(1)} %get-tuple-element.71) | copy-start | bytes 4718596
  343.8 134.8 %reduce-scatter.15.cloned.1.call-start = ((), (), s32[]{:S(2)}) async-start(), calls=%async_computation.12 | async-start | bytes 3760128 | tf_op jit(solution)/shard_map/reduce_scatter | solution.py:47
  355.6 201.4 %reduce-scatter.23.cloned.1.call-start = ((), (), s32[]{:S(2)}) async-start(), calls=%async_computation.16 | async-start | bytes 5013504 | tf_op jit(solution)/shard_map/reduce_scatter | solution.py:47
  356.4 279.3 %reduce-scatter.19.cloned.1.call-start = ((), (), s32[]{:S(2)}) async-start(), calls=%async_computation.14 | async-start | bytes 5013504 | tf_op jit(solution)/shard_map/reduce_scatter | solution.py:47
  364.7 116.0 %all-to-all-start.1 = ((bf16[16,32,768]{2,1,0:T(8,128)(2,1)}), bf16[16,32,768]{2,1,0:T(8,128)(2,1)S(1)}, u32[]{:S(2)}, u32[]{:S(2)}) async-start(bf16[16,32,768]{2,1,0:T(8,128)(2,1)} %bitcast.19), calls=%async_computation.1 | async-start | bytes 1572864 | tf_op jit(solution)/shard_map/all_to_all | solution.py:145
  368.6 332.2 %reduce-scatter.27.cloned.1.call-start = ((), (), s32[]{:S(2)}) async-start(), calls=%async_computation.22 | async-start | bytes 294912
  409.5 292.9 %reduce-scatter.25.cloned.1.call-start = ((), (), s32[]{:S(2)}) async-start(), calls=%async_computation.21 | async-start | bytes 884736
  480.6 220.1 %all-to-all-start.3 = ((bf16[16,32,768]{2,1,0:T(8,128)(2,1)}), bf16[16,32,768]{2,1,0:T(8,128)(2,1)S(1)}, u32[]{:S(2)}, u32[]{:S(2)}) async-start(bf16[16,32,768]{2,1,0:T(8,128)(2,1)} %bitcast.32), calls=%async_computation.3 | async-start | bytes 1572864 | tf_op jit(solution)/shard_map/all_to_all | solution.py:196
  484.3 220.0 %reduce-scatter.29.cloned.1.call-start = ((), (), s32[]{:S(2)}) async-start(), calls=%async_computation.23 | async-start | bytes 589824
  558.9 147.2 %reduce-scatter.21.cloned.1.call-start = ((), (), s32[]{:S(2)}) async-start(), calls=%async_computation.15 | async-start | bytes 442368 | tf_op jit(solution)/shard_map/reduce_scatter | solution.py:48
  636.5 4.1 collective-permute-start
  (28 other events, 265.1 us)
Sparse Core Ops, SparseCore 0:
  11.0 62.0 all-gather.11
  76.0 59.8 all-gather.9
  138.8 62.2 all-gather.13
  203.9 61.8 all-gather.15
  343.9 63.8 reduce-scatter.16
  411.5 67.0 reduce-scatter.14
  482.5 74.4 reduce-scatter.22
  560.8 74.8 reduce-scatter.18
  638.5 10.1 reduce-scatter.26
  651.4 15.3 reduce-scatter.24
  669.6 13.1 reduce-scatter.28
  684.9 12.0 reduce-scatter.20
where the time goes:
time: 720 us; the launch traced here: 717 us
  waiting for transfers between devices  385 us (53%)
  blocking collectives  126 us (18%)
  matrix products  75.5 us (10%)
  local copies, waits for them, and re-layouts  66.3 us (9%)
  other arithmetic  25.1 us (3%)
  starting transfers between devices  22.8 us (3%)
  between operations  15.8 us (2%)
    reduce_scatter x4, waiting for transfers between devices, scatter_matrix(): lax.psum_scatter(grad.astype(jnp.bfloat16), 'dp', scatter_dimension=0, ti...  258 us
    unnamed x2, blocking collectives  126 us
    all_gather x4, waiting for transfers between devices, gather_matrix(): every = lax.all_gather(block, ('dp', 'fsdp'), axis=0, tiled=False)  106 us
    dot_general x14, matrix products, matmul(): jnp.einsum(pattern, left_side, right_side, preferred_element_type=jnp.flo...  63 us
    unnamed x85, local copies, waits for them, and re-layouts  27 us
    reshape x4, local copies, waits for them, and re-layouts, gather_matrix(): every = every.reshape(n_dp, n_fsdp, rows, cols).transpose(0, 2, 1, 3)  25.9 us
    all_to_all x1, waiting for transfers between devices, local(): lax.all_to_all(patches, 'dp', split_axis=0, concat_axis=0, tiled=True)  14.6 us
  transfers between devices with their start and end apart: 17, of which 9 were waited for; matrix products, arithmetic and copies ran while one was open for 12% of the time, Pallas kernels for 0%

commit v1 on v0

--- a/solution.py
+++ b/solution.py
@@ -8,6 +8,25 @@
 NORM_EPSILON = 1e-12
 MASK_VALUE = -1e30
 ROOT_HALF = 0.7071067811865476
+
+
+def sides_refer(point):
+    state_now = lax.axis_size("dp")
+    long_array, reached = (state_now, lax.axis_index("dp"))
+    local_part = point.shape[0] // long_array
+    w2 = jnp.roll(point, -reached * local_part, 0)
+    carry_out = lax.slice_in_dim(w2, 0, local_part, axis=0)
+    series = [carry_out]
+    no = 1
+    while no < long_array:
+        local_now = lax.slice_in_dim(w2, no * local_part, (no + 1) * local_part, axis=0)
+        series.append(
+            lax.ppermute(local_now, "dp", [(c, (c + no) % long_array) for c in range(long_array)])
+        )
+        no += 1
+    taken_in = jnp.concatenate(series[::-1], axis=0)
+    z = jnp.roll(taken_in, (reached + 1) * series[0].shape[0], axis=0)
+    return z
 
 
 def norm_rows(values, norm_gain, norm_shift):
@@ -71,7 +90,7 @@
     down_bias,
 ):
     arrived, cot_rows = (
-        lax.all_to_all(patches, "dp", split_axis=0, concat_axis=0, tiled=True),
+        sides_refer(patches),
         lax.all_to_all(cotangent, "dp", split_axis=0, concat_axis=0, tiled=True),
     )
     total_rows, width = patches.shape

time: 720 us -> 686 us (0.953)
  waiting for transfers between devices: 385 us -> 315 us
  starting transfers between devices: 22.8 us -> 51.7 us
  local copies, waits for them, and re-layouts: 66.3 us -> 74.6 us
    all_gather x4, waiting for transfers between devices: 106 us -> 63.4 us  [gather_matrix(): every = lax.all_gather(block, ('dp', 'fsdp'), axis=0, tiled=False)]
    reduce_scatter x4, waiting for transfers between devices: 258 us -> 220 us  [scatter_matrix(): lax.psum_scatter(grad.astype(jnp.bfloat16), 'dp', scatter_dimension=0, ti...]
    ppermute x0 -> x15, starting transfers between devices: none -> 34.4 us  [sides_refer(): lax.ppermute(local_now, 'dp', [(c, (c + no) % long_array) for c in range(...]
    ppermute x0 -> x15, waiting for transfers between devices: none -> 25.1 us  [sides_refer(): lax.ppermute(local_now, 'dp', [(c, (c + no) % long_array) for c in range(...]
    all_to_all x1 -> x0, waiting for transfers between devices: 14.6 us -> none  [local(): lax.all_to_all(patches, 'dp', split_axis=0, concat_axis=0, tiled=True)]
    all_to_all x1 -> x0, starting transfers between devices: 7.43 us -> none  [local(): lax.all_to_all(patches, 'dp', split_axis=0, concat_axis=0, tiled=True)]
    unnamed x85 -> x128, local copies, waits for them, and re-layouts: 27 us -> 30 us
  transfers between devices with their start and end apart: 17 -> 31, of which waited for: 9 -> 17; matrix products, arithmetic and copies ran while one was open for 12% -> 18% of each run, Pallas kernels for 0% -> 0%
where the time goes in v1:
time: 686 us; the launch traced here: 680 us
  waiting for transfers between devices  315 us (46%)
  blocking collectives  121 us (18%)
  local copies, waits for them, and re-layouts  74.6 us (11%)
  matrix products  72.7 us (11%)
  starting transfers between devices  51.7 us (8%)
  other arithmetic  29.4 us (4%)
  between operations  16.2 us (2%)
    reduce_scatter x4, waiting for transfers between devices, scatter_matrix(): lax.psum_scatter(grad.astype(jnp.bfloat16), 'dp', scatter_dimension=0, ti...  220 us
    unnamed x2, blocking collectives  121 us
    all_gather x4, waiting for transfers between devices, gather_matrix(): every = lax.all_gather(block, ('dp', 'fsdp'), axis=0, tiled=False)  63.4 us
    dot_general x14, matrix products, matmul(): jnp.einsum(pattern, left_side, right_side, preferred_element_type=jnp.flo...  59.6 us
    ppermute x15, starting transfers between devices, sides_refer(): lax.ppermute(local_now, 'dp', [(c, (c + no) % long_array) for c in range(...  34.4 us
    unnamed x128, local copies, waits for them, and re-layouts  30 us
    reshape x4, local copies, waits for them, and re-layouts, gather_matrix(): every = every.reshape(n_dp, n_fsdp, rows, cols).transpose(0, 2, 1, 3)  25.9 us
    ppermute x15, waiting for transfers between devices, sides_refer(): lax.ppermute(local_now, 'dp', [(c, (c + no) % long_array) for c in range(...  25.1 us
  transfers between devices with their start and end apart: 31, of which 17 were waited for; matrix products, arithmetic and copies ran while one was open for 18% of the time, Pallas kernels for 0%

profile of v1, /device:TPU:0, one launch (start us, length us, event | category | flops | bytes accessed | tf_op | source)
XLA Modules:
  0.0 680.3 jit_solution(10080293573523621707)
XLA Ops:
  9.5 7.6 %all-to-all-start.1 = ((bf16[16,32,768]{2,1,0:T(8,128)(2,1)}), bf16[16,32,768]{2,1,0:T(8,128)(2,1)S(1)}, u32[]{:S(2)}, u32[]{:S(2)}) async-start(bf16[16,32,768]{2,1,0:T(8,128)(2,1)} %bitcast.137), calls=%async_computation.1 | async-start | bytes 1572864 | tf_op jit(solution)/shard_map/all_to_all | solution.py:94
  28.0 63.1 %all-reduce = bf16[9216]{0:T(1024)(128)(2,1)S(1)} all-reduce(bf16[9216]{0:T(1024)(128)(2,1)S(1)} %dynamic-update-slice), channel_id=2, replica_groups=mesh['dp'=16,'fsdp'=2] {'dp'}, use_global_device_ids=true, to_apply=%add | all-reduce | flops 9216 | bytes 36864
  109.0 4.3 collective-permute-done.3
  117.0 4.6 collective-permute-start.5
  123.4 6.8 %collective-permute-start.6 = (bf16[32,768]{1,0:T(8,128)(2,1)S(1)}, bf16[32,768]{1,0:T(8,128)(2,1)S(1)}, u32[]{:S(2)}, u32[]{:S(2)}) collective-permute-start(bf16[32,768]{1,0:T(8,128)(2,1)S(1)} %get-tuple-element.56), channel_id=1, source_target_pairs={{0,18},{2,20},{4,22},{6,24},{8,26},{10,28},{12,30},{14,0},{16,2},{... | collective-permute-start | bytes 147464 | tf_op jit(solution)/shard_map/ppermute | solution.py:24
  141.7 4.7 collective-permute-start.9
  160.5 4.8 copy.68
  185.5 13.8 %all-gather.14.cloned.1.call-done = bf16[1536,1536]{1,0:T(8,128)(2,1)} async-done(((bf16[48,1536]{1,0:T(8,128)(2,1)}), bf16[1536,1536]{1,0:T(8,128)(2,1)}) %all-gather.14.cloned.1.call-update) | async-done | bytes 4718608 | tf_op jit(solution)/shard_map/all_gather | solution.py:60
  199.3 9.4 %copy.74 = bf16[16,2,48,1536]{3,1,2,0:T(2,128)(2,1)} copy(bf16[16,2,48,1536]{3,2,1,0:T(8,128)(2,1)} %bitcast.112) | data formatting | bytes 9437184 | tf_op jit(solution)/shard_map/reshape | solution.py:61
  208.7 5.7 copy.92
  214.5 49.5 %all-gather.16.cloned.1.call-done = bf16[6144,384]{1,0:T(8,128)(2,1)} async-done(((bf16[192,384]{1,0:T(8,128)(2,1)}), bf16[6144,384]{1,0:T(8,128)(2,1)}) %all-gather.16.cloned.1.call-update) | async-done | bytes 4718608 | tf_op jit(solution)/shard_map/all_gather | solution.py:60
  264.0 9.5 %copy.75 = bf16[16,2,192,384]{3,1,2,0:T(2,128)(2,1)} copy(bf16[16,2,192,384]{3,2,1,0:T(8,128)(2,1)} %bitcast.113) | data formatting | bytes 9437184 | tf_op jit(solution)/shard_map/reshape | solution.py:61
  280.1 6.6 convert_reduce_fusion
  290.7 4.9 convolution_convert_fusion.1
  299.7 4.5 convolution_convert_fusion.2
  311.4 13.5 %multiply_reduce_fusion = (f32[12,512]{1,0:T(8,128)S(1)}, f32[12,512,512]{1,2,0:T(8,128)}) fusion(f32[12,512]{1,0:T(8,128)S(1)} %log_add_fusion, f32[12,512,512]{1,2,0:T(8,128)} %copy-done, pred[512,512]{0,1:T(8,128)(4,1)S(1)} %broadcast_compare_fusion, bf16[512,12,64]{0,2,1:T(8,128)(2,1)} %bitcast.124, bf16[512,12,64]{0,2,1:T(8,128)(2,1)} %bitcast.123), kind=kOutput, calls=%fused_computation.2 | convolution fusion | flops 418375680 | bytes 27049984 | tf_op jit(solution)/shard_map/qhe,khe->hqk/dot_general | solution.py:51
  324.9 10.8 %multiply_convert_fusion = bf16[12,512,512]{1,2,0:T(8,128)(2,1)S(1)} fusion(f32[12,512,512]{1,2,0:T(8,128)} %get-tuple-element.87, f32[12,512]{1,0:T(8,128)S(1)} %get-tuple-element.86, f32[12,512]{1,0:T(8,128)S(1)} %log_add_fusion, f32[12,512,512]{1,2,0:T(8,128)} %copy-done, pred[512,512]{0,1:T(8,128)(4,1)S(1)} %broadcast_compare_fusion), kind=kLoop, calls=%fused_computation.1 | loop fusion | flops 18874368 | bytes 31768576 | tf_op jit(solution)/shard_map/convert_element_type | solution.py:200
  348.2 7.3 %multiply_convert_fusion.5 = bf16[512,768]{1,0:T(8,128)(2,1)} fusion(f32[512,768]{1,0:T(8,128)} %copy-done.5, bf16[512,3072]{1,0:T(8,128)(2,1)} %get-tuple-element.41, bf16[3072,768]{1,0:T(8,128)(2,1)} %bitcast.115, f32[768]{0:T(1024)S(1)} %reshape.365, f32[512]{0:T(512)S(1)} %copy-done.24), kind=kOutput, calls=%fused_computation.58 | convolution fusion | flops 2417491968 | bytes 10228736 | tf_op jit(solution)/shard_map/dot_general | solution.py:162
  359.7 5.1 fusion.45
  366.8 4.3 reduce-scatter.17.cloned.1.call-done
  372.8 69.3 %reduce-scatter.15.cloned.1.call-done = bf16[48,2304]{1,0:T(8,128)(2,1)} async-done(((bf16[768,2304]{1,0:T(8,128)(2,1)}), bf16[48,2304]{1,0:T(8,128)(2,1)}) %reduce-scatter.15.cloned.1.call-update) | async-done | bytes 221200 | tf_op jit(solution)/shard_map/reduce_scatter | solution.py:66
  450.7 69.9 %reduce-scatter.23.cloned.1.call-done = bf16[192,768]{1,0:T(8,128)(2,1)} async-done(((bf16[3072,768]{1,0:T(8,128)(2,1)}), bf16[192,768]{1,0:T(8,128)(2,1)}) %reduce-scatter.23.cloned.1.call-update) | async-done | bytes 294928 | tf_op jit(solution)/shard_map/reduce_scatter | solution.py:66
  522.5 76.8 %reduce-scatter.19.cloned.1.call-done = bf16[48,3072]{1,0:T(8,128)(2,1)} async-done(((bf16[768,3072]{1,0:T(8,128)(2,1)}), bf16[48,3072]{1,0:T(8,128)(2,1)}) %reduce-scatter.19.cloned.1.call-update) | async-done | bytes 294928 | tf_op jit(solution)/shard_map/reduce_scatter | solution.py:66
  604.1 57.7 %all-reduce.1 = f32[16,576]{1,0:T(8,128)S(1)} all-reduce(f32[16,576]{1,0:T(8,128)S(1)} %add.165), channel_id=7, replica_groups=mesh['dp'=16,'fsdp'=2] {'dp'}, use_global_device_ids=true, to_apply=%region_23.25.clone | all-reduce | flops 9216 | bytes 73728
  (268 shorter events, 149.6 us)
Async XLA Ops:
  7.2 149.9 %all-gather.12.cloned.1.call-start = ((), (), s32[]{:S(2)}) async-start(), calls=%async_computation.17 | async-start | bytes 1216512 | tf_op jit(solution)/shard_map/all_gather | solution.py:60
  7.9 152.6 %all-gather.10.cloned.1.call-start = ((), (), s32[]{:S(2)}) async-start(), calls=%async_computation.16 | async-start | bytes 3649536 | tf_op jit(solution)/shard_map/all_gather | solution.py:60
  8.7 190.7 %all-gather.14.cloned.1.call-start = ((), (), s32[]{:S(2)}) async-start(), calls=%async_computation.18 | async-start | bytes 4866048 | tf_op jit(solution)/shard_map/all_gather | solution.py:60
  9.5 146.3 %all-to-all-start.1 = ((bf16[16,32,768]{2,1,0:T(8,128)(2,1)}), bf16[16,32,768]{2,1,0:T(8,128)(2,1)S(1)}, u32[]{:S(2)}, u32[]{:S(2)}) async-start(bf16[16,32,768]{2,1,0:T(8,128)(2,1)} %bitcast.137), calls=%async_computation.1 | async-start | bytes 1572864 | tf_op jit(solution)/shard_map/all_to_all | solution.py:94
  17.1 246.9 %all-gather.16.cloned.1.call-start = ((), (), s32[]{:S(2)}) async-start(), calls=%async_computation.19 | async-start | bytes 4866048 | tf_op jit(solution)/shard_map/all_gather | solution.py:60
  18.3 136.6 %collective-permute-start.14 = (bf16[32,768]{1,0:T(8,128)(2,1)S(1)}, bf16[32,768]{1,0:T(8,128)(2,1)S(1)}, u32[]{:S(2)}, u32[]{:S(2)}) collective-permute-start(bf16[32,768]{1,0:T(8,128)(2,1)S(1)} %get-tuple-element.48), channel_id=1, source_target_pairs={{0,2},{2,4},{4,6},{6,8},{8,10},{10,12},{12,14},{14,16},{16,18},{18... | collective-permute-start | bytes 147464 | tf_op jit(solution)/shard_map/ppermute | solution.py:24
  18.7 136.1 %collective-permute-start.13 = (bf16[32,768]{1,0:T(8,128)(2,1)S(1)}, bf16[32,768]{1,0:T(8,128)(2,1)S(1)}, u32[]{:S(2)}, u32[]{:S(2)}) collective-permute-start(bf16[32,768]{1,0:T(8,128)(2,1)S(1)} %get-tuple-element.49), channel_id=1, source_target_pairs={{0,4},{2,6},{4,8},{6,10},{8,12},{10,14},{12,16},{14,18},{16,20},{1... | collective-permute-start | bytes 147464 | tf_op jit(solution)/shard_map/ppermute | solution.py:24
  20.4 134.5 %collective-permute-start.12 = (bf16[32,768]{1,0:T(8,128)(2,1)S(1)}, bf16[32,768]{1,0:T(8,128)(2,1)S(1)}, u32[]{:S(2)}, u32[]{:S(2)}) collective-permute-start(bf16[32,768]{1,0:T(8,128)(2,1)S(1)} %get-tuple-element.50), channel_id=1, source_target_pairs={{0,6},{2,8},{4,10},{6,12},{8,14},{10,16},{12,18},{14,20},{16,22},{... | collective-permute-start | bytes 147464 | tf_op jit(solution)/shard_map/ppermute | solution.py:24
  22.6 131.4 %collective-permute-start.11 = (bf16[32,768]{1,0:T(8,128)(2,1)S(1)}, bf16[32,768]{1,0:T(8,128)(2,1)}, u32[]{:S(2)}, u32[]{:S(2)}) collective-permute-start(bf16[32,768]{1,0:T(8,128)(2,1)S(1)} %get-tuple-element.51), channel_id=1, source_target_pairs={{0,8},{2,10},{4,12},{6,14},{8,16},{10,18},{12,20},{14,22},{16,24},... | collective-permute-start | bytes 147464 | tf_op jit(solution)/shard_map/ppermute | solution.py:24
  24.1 76.7 %collective-permute-start = (bf16[32,768]{1,0:T(8,128)(2,1)S(1)}, bf16[32,768]{1,0:T(8,128)(2,1)S(1)}, u32[]{:S(2)}, u32[]{:S(2)}) collective-permute-start(bf16[32,768]{1,0:T(8,128)(2,1)S(1)} %get-tuple-element.62), channel_id=1, source_target_pairs={{0,30},{2,0},{4,2},{6,4},{8,6},{10,8},{12,10},{14,12},{16,14},{18,... | collective-permute-start | bytes 147464 | tf_op jit(solution)/shard_map/ppermute | solution.py:24
  26.0 345.0 %reduce-scatter.17.cloned.1.call-start = ((), (), s32[]{:S(2)}) async-start(), calls=%async_computation.12 | async-start | bytes 1253376 | tf_op jit(solution)/shard_map/reduce_scatter | solution.py:66
  117.0 6.4 collective-permute-start.5
  123.4 8.6 %collective-permute-start.6 = (bf16[32,768]{1,0:T(8,128)(2,1)S(1)}, bf16[32,768]{1,0:T(8,128)(2,1)S(1)}, u32[]{:S(2)}, u32[]{:S(2)}) collective-permute-start(bf16[32,768]{1,0:T(8,128)(2,1)S(1)} %get-tuple-element.56), channel_id=1, source_target_pairs={{0,18},{2,20},{4,22},{6,24},{8,26},{10,28},{12,30},{14,0},{16,2},{... | collective-permute-start | bytes 147464 | tf_op jit(solution)/shard_map/ppermute | solution.py:24
  141.7 6.5 collective-permute-start.9
  148.2 5.9 collective-permute-start.10
  311.3 130.8 %reduce-scatter.15.cloned.1.call-start = ((), (), s32[]{:S(2)}) async-start(), calls=%async_computation.11 | async-start | bytes 3760128 | tf_op jit(solution)/shard_map/reduce_scatter | solution.py:66
  346.6 173.9 %reduce-scatter.23.cloned.1.call-start = ((), (), s32[]{:S(2)}) async-start(), calls=%async_computation.15 | async-start | bytes 5013504 | tf_op jit(solution)/shard_map/reduce_scatter | solution.py:66
  347.4 251.8 %reduce-scatter.19.cloned.1.call-start = ((), (), s32[]{:S(2)}) async-start(), calls=%async_computation.13 | async-start | bytes 5013504 | tf_op jit(solution)/shard_map/reduce_scatter | solution.py:66
  355.5 91.5 %all-to-all-start = ((bf16[16,32,768]{2,1,0:T(8,128)(2,1)}), bf16[16,32,768]{2,1,0:T(8,128)(2,1)S(1)}, u32[]{:S(2)}, u32[]{:S(2)}) async-start(bf16[16,32,768]{2,1,0:T(8,128)(2,1)} %bitcast.139), calls=%async_computation | async-start | bytes 1572864 | tf_op jit(solution)/shard_map/all_to_all | solution.py:164
  359.4 304.9 %reduce-scatter.27.cloned.1.call-start = ((), (), s32[]{:S(2)}) async-start(), calls=%async_computation.21 | async-start | bytes 294912
  372.8 293.2 %reduce-scatter.25.cloned.1.call-start = ((), (), s32[]{:S(2)}) async-start(), calls=%async_computation.20 | async-start | bytes 884736
  447.0 217.3 %all-to-all-start.2 = ((bf16[16,32,768]{2,1,0:T(8,128)(2,1)}), bf16[16,32,768]{2,1,0:T(8,128)(2,1)S(1)}, u32[]{:S(2)}, u32[]{:S(2)}) async-start(bf16[16,32,768]{2,1,0:T(8,128)(2,1)} %bitcast.29), calls=%async_computation.2 | async-start | bytes 1572864 | tf_op jit(solution)/shard_map/all_to_all | solution.py:215
  450.6 217.2 %reduce-scatter.29.cloned.1.call-start = ((), (), s32[]{:S(2)}) async-start(), calls=%async_computation.22 | async-start | bytes 589824
  522.4 147.2 %reduce-scatter.21.cloned.1.call-start = ((), (), s32[]{:S(2)}) async-start(), calls=%async_computation.14 | async-start | bytes 442368 | tf_op jit(solution)/shard_map/reduce_scatter | solution.py:67
  (56 other events, 550.1 us)
Sparse Core Ops, SparseCore 0:
  10.9 58.9 all-gather.11
  72.9 59.6 all-gather.9
  135.5 63.7 all-gather.13
  202.1 61.8 all-gather.15
  311.5 59.5 reduce-scatter.16
  374.8 67.3 reduce-scatter.14
  446.0 74.5 reduce-scatter.22
  524.4 74.8 reduce-scatter.18
  602.0 10.2 reduce-scatter.26
  614.4 15.3 reduce-scatter.24
  632.6 13.1 reduce-scatter.28
  647.9 12.1 reduce-scatter.20
